TPU v7x, 256 devices: a whole 4x4x8 slice. The times are simulated.
256 devices in a mesh: section: 8 (over z), col: 32 (over y, x, core).
Axes of the slice: x: 4, y: 4, z: 8, core: 2. Of those that a mesh axis runs over, the one named last changes fastest.
Arguments:
- tiles: bfloat16 [1024, 12, 128, 128], P('col', None, 'section'), may hold values from 0.0099487305 to 1
- offsets: int32 [1024, 12], replicated, may hold values from -6 to 6, as said below
- counts: int32 [1024], replicated, may hold values from 1 to 12
- ranks: int32 [1024, 25, 128, 128], P('col', None, 'section'), may hold values from 0 to 3199, as said below
Outputs:
- pruned: bfloat16 [1024, 25, 128, 128], P('col', None, 'section')
Inputs may be any that keep to these rules, and one draw needn't show every extreme that they name: Within each panel the 12 offsets are distinct, each from -6 to 6. For every panel j and column c, ranks[j, :, c, :] holds each of 0 .. 3199 once.
All inputs are finite; a program needn't handle non-finite values.
Results may differ from a plain program's by a relative error of at most 0.001.
Values may be sent and summed in bfloat16 or wider, within the bound.
A program may use at most 128 MiB of HBM per device.

v0:
```python
import jax
import jax.numpy as jnp
from jax import lax
from jax.sharding import PartitionSpec as P

W = 6
TOPK = 256


def extended(shard, sides, width):
    for axis, dim in sides:
        count, length = (lax.axis_size(axis), shard.shape[dim])
        up = [(i, (i + 1) % count) for i in range(count - 1)]
        down = [(j, i) for i, j in up]
        last = lax.slice_in_dim(shard, length - width, length, axis=dim)
        initial = lax.slice_in_dim(shard, 0, width, axis=dim)
        before = lax.ppermute(last, axis, up)
        after = lax.ppermute(initial, axis, down)
        shard = jnp.concatenate([before, shard, after], axis=dim)
    return shard


def cut_along(shard, dim, count):
    before, after = (shard.shape[:dim], shard.shape[dim + 1 :])
    return jnp.moveaxis(shard.reshape(*before, count, -1, *after), dim, 0)


def piece_ends(length, count):
    unit = 8 if length >= 8 * count else 1
    return [length // unit * k // count * unit for k in range(1, count)]


def joined_along(tiles, dim):
    tiles = jnp.moveaxis(tiles, 0, dim)
    dims = tiles.shape
    return tiles.reshape(*dims[:dim], dims[dim] * dims[dim + 1], *dims[dim + 2 :])


def exchange_in_pieces(shard, axis, pieces, split_dim, concat_dim):
    tiles = cut_along(shard, split_dim, lax.axis_size(axis))
    split_at = max(range(1, max(2, tiles.ndim - 1)), key=lambda d: tiles.shape[d])
    outs = []
    for share in jnp.split(tiles, piece_ends(tiles.shape[split_at], pieces), axis=split_at):
        if share.size:
            outs.append(lax.all_to_all(share, axis, split_axis=0, concat_axis=0, tiled=True))
    return joined_along(jnp.concatenate(outs, axis=split_at), concat_dim)


def expand(own, own_off, own_cnt, center, global_panel, banded, band_off, band_cnt, total, bands):
    slots = own.shape[0]
    slot_ids = jnp.arange(slots, dtype=jnp.int32)
    where_at = center + W + own_off
    firsts = banded[where_at]
    first_off = band_off[where_at]
    first_cnt = band_cnt[where_at]
    row_own = global_panel + own_off
    ok_own = (slot_ids < own_cnt) & (row_own >= 0) & (row_own < total)
    row_first = row_own[:, None] + first_off
    ok_first = (slot_ids[None, :] < first_cnt[:, None]) & (row_first >= 0) & (row_first < total)
    weight = (ok_own[:, None] & ok_first).astype(jnp.float32)
    target = own_off[:, None] + first_off + 2 * W
    products = jnp.einsum("kcx,klxr->klcr", own, firsts, preferred_element_type=jnp.float32)
    weighted = products * weight[:, :, None, None]
    columns = own.shape[1]
    rows = own.shape[2]
    empty = jnp.zeros((bands, columns, rows), jnp.float32)
    return empty.at[target.reshape(-1)].add(weighted.reshape((slots * slots, columns, rows)))


def finish(expanded, rank_block):
    keep = rank_block < TOPK
    squared = jnp.where(keep, expanded * expanded, jnp.float32(0.0))
    totals = jnp.sum(squared, axis=(0, 2), keepdims=True)
    return (TOPK * squared / (totals + 1e-06)).astype(jnp.bfloat16)


def shards(tiles, offsets, counts, ranks):
    panels = tiles.shape[0]
    slots = tiles.shape[1]
    bands = ranks.shape[1]
    total = offsets.shape[0]
    first_panel = lax.axis_index("col") * panels
    pad_off = jnp.concatenate(
        [jnp.zeros((W, slots), jnp.int32), offsets, jnp.zeros((W, slots), jnp.int32)], axis=0
    )
    pad_cnt = jnp.concatenate(
        [jnp.zeros((W,), jnp.int32), counts, jnp.zeros((W,), jnp.int32)], axis=0
    )
    sections = lax.axis_size("section")
    share = panels // sections
    start = first_panel + lax.axis_index("section") * share
    sliced = extended(tiles, (("col", 0),), W)
    windows = jnp.stack([sliced[t * share : t * share + share + 2 * W] for t in range(sections)], 0)
    whole = lax.all_to_all(windows, "section", split_axis=0, concat_axis=3, tiled=True)[0]
    win_off = lax.dynamic_slice_in_dim(pad_off, start, share + 2 * W, 0)
    win_cnt = lax.dynamic_slice_in_dim(pad_cnt, start, share + 2 * W, 0)
    loc_off = lax.dynamic_slice_in_dim(offsets, start, share, 0)
    loc_cnt = lax.dynamic_slice_in_dim(counts, start, share, 0)

    def one_whole(packed):
        p_off, p_cnt, centre = packed
        own = lax.dynamic_index_in_dim(whole, centre + W, 0, False)
        return expand(
            own, p_off, p_cnt, centre, start + centre, whole, win_off, win_cnt, total, bands
        )

    expanded = lax.map(one_whole, (loc_off, loc_cnt, jnp.arange(share, dtype=jnp.int32)))
    back = exchange_in_pieces(expanded, "section", 2, 2, 0)

    def one_finish(packed):
        values, rank_block = packed
        return finish(values, rank_block)

    return lax.map(one_finish, (back, ranks))


def solution(mesh):
    placed = (P("col", None, "section", None), P(), P(), P("col", None, "section", None))
    return jax.shard_map(
        shards,
        mesh=mesh,
        in_specs=placed,
        out_specs=P("col", None, "section", None),
        check_vma=False,
    )
```

profile of v0, /device:TPU:14, one launch (start us, length us, event | category | flops | bytes accessed | tf_op | source)
XLA Modules:
  0.0 642.6 jit_solution(12305052271781320024)
XLA Ops:
  19.7 8.6 %all-to-all-start = ((bf16[8,16,12,16,128]{4,3,2,1,0:T(8,128)(2,1)}), bf16[8,16,12,16,128]{4,3,2,1,0:T(8,128)(2,1)}, u32[]{:S(2)}, u32[]{:S(2)}) async-start(bf16[8,16,12,16,128]{4,3,2,1,0:T(8,128)(2,1)} %fusion.11), calls=%async_computation | async-start | bytes 12582912 | tf_op jit(solution)/shard_map/all_to_all | solution.py:94
  29.0 140.1 %all-to-all-done = bf16[8,16,12,16,128]{4,3,2,1,0:T(8,128)(2,1)} async-done(((bf16[8,16,12,16,128]{4,3,2,1,0:T(8,128)(2,1)}), bf16[8,16,12,16,128]{4,3,2,1,0:T(8,128)(2,1)}, u32[]{:S(2)}, u32[]{:S(2)}) %all-to-all-start) | async-done | bytes 6291488 | tf_op jit(solution)/shard_map/all_to_all | solution.py:94
  169.1 7.3 %copy.20 = bf16[1,16,12,8,16,128]{5,4,3,2,1,0:T(8,128)(2,1)} copy(bf16[1,16,12,8,16,128]{5,4,2,1,3,0:T(8,128)(2,1)} %bitcast.21) | data formatting | bytes 12582912 | tf_op jit(solution)/shard_map/all_to_all | solution.py:94
  176.4 199.5 %while.22 = (s32[]{:T(128)}, f32[4,25,128,128]{3,2,1,0:T(8,128)}, s32[4,12]{1,0:T(4,128)S(1)}, s32[4]{0:T(128)S(1)}, s32[16,12]{1,0:T(8,128)S(1)}, /*index=5*/bf...) while((s32[]{:T(128)}, f32[4,25,128,128]{3,2,1,0:T(8,128)}, ...), condition=%wide.region_2.3_spmd, body=%wide.region_0.2_spmd.sunk | while | flops 608701376 | bytes 76102056 | solution.py:107
  181.4 6.3 gather_fusion.2
  187.7 8.0 %broadcast_multiply_fusion.2 = f32[12,12,128,128]{3,2,1,0:T(8,128)} fusion(f32[12,12]{1,0:T(8,128)S(1)} %fusion.27, bf16[12,12,128,128]{3,2,1,0:T(8,128)(2,1)} %gather_fusion.2, bf16[16,12,128,128]{3,2,1,0:T(8,128)(2,1)} %get-tuple-element.310, s32[]{:T(128)S(6)} %select_n.67), kind=kOutput, calls=%fused_computation.10.clone.1 | convolution fusion | flops 606339072 | bytes 14549572 | tf_op jit(solution)/shard_map/while/body/eval_jaxpr/kcx,klxr->klcr/dot_general | solution.py:62
  195.8 9.6 %copy.29 = f32[144,128,128]{2,1,0:T(8,128)} copy(f32[144,128,128]{1,2,0:T(8,128)} %bitcast.73) | data formatting | bytes 18874368 | tf_op jit(solution)/shard_map/while/body/eval_jaxpr/reshape | solution.py:67
  205.8 19.1 %scatter_fusion = f32[25,128,128]{2,1,0:T(8,128)S(1)} fusion(f32[25,128,128]{2,1,0:T(8,128)S(1)} %broadcast.274, s32[144]{0:T(256)S(1)} %bitcast.79, f32[144,128,128]{2,1,0:T(8,128)} %copy.29), kind=kCustom, calls=%fused_computation.3.clone.1 | custom fusion | flops 2359296 | bytes 28312128 | tf_op jit(solution)/shard_map/while/body/eval_jaxpr/scatter-add | solution.py:67
  231.3 6.3 gather_fusion.2
  237.6 8.0 %broadcast_multiply_fusion.2 = f32[12,12,128,128]{3,2,1,0:T(8,128)} fusion(f32[12,12]{1,0:T(8,128)S(1)} %fusion.27, bf16[12,12,128,128]{3,2,1,0:T(8,128)(2,1)} %gather_fusion.2, bf16[16,12,128,128]{3,2,1,0:T(8,128)(2,1)} %get-tuple-element.310, s32[]{:T(128)S(6)} %select_n.67), kind=kOutput, calls=%fused_computation.10.clone.1 | convolution fusion | flops 606339072 | bytes 14549572 | tf_op jit(solution)/shard_map/while/body/eval_jaxpr/kcx,klxr->klcr/dot_general | solution.py:62
  245.6 9.6 %copy.29 = f32[144,128,128]{2,1,0:T(8,128)} copy(f32[144,128,128]{1,2,0:T(8,128)} %bitcast.73) | data formatting | bytes 18874368 | tf_op jit(solution)/shard_map/while/body/eval_jaxpr/reshape | solution.py:67
  255.6 19.1 %scatter_fusion = f32[25,128,128]{2,1,0:T(8,128)S(1)} fusion(f32[25,128,128]{2,1,0:T(8,128)S(1)} %broadcast.274, s32[144]{0:T(256)S(1)} %bitcast.79, f32[144,128,128]{2,1,0:T(8,128)} %copy.29), kind=kCustom, calls=%fused_computation.3.clone.1 | custom fusion | flops 2359296 | bytes 28312128 | tf_op jit(solution)/shard_map/while/body/eval_jaxpr/scatter-add | solution.py:67
  281.1 6.3 gather_fusion.2
  287.4 8.0 %broadcast_multiply_fusion.2 = f32[12,12,128,128]{3,2,1,0:T(8,128)} fusion(f32[12,12]{1,0:T(8,128)S(1)} %fusion.27, bf16[12,12,128,128]{3,2,1,0:T(8,128)(2,1)} %gather_fusion.2, bf16[16,12,128,128]{3,2,1,0:T(8,128)(2,1)} %get-tuple-element.310, s32[]{:T(128)S(6)} %select_n.67), kind=kOutput, calls=%fused_computation.10.clone.1 | convolution fusion | flops 606339072 | bytes 14549572 | tf_op jit(solution)/shard_map/while/body/eval_jaxpr/kcx,klxr->klcr/dot_general | solution.py:62
  295.5 9.6 %copy.29 = f32[144,128,128]{2,1,0:T(8,128)} copy(f32[144,128,128]{1,2,0:T(8,128)} %bitcast.73) | data formatting | bytes 18874368 | tf_op jit(solution)/shard_map/while/body/eval_jaxpr/reshape | solution.py:67
  305.5 19.1 %scatter_fusion = f32[25,128,128]{2,1,0:T(8,128)S(1)} fusion(f32[25,128,128]{2,1,0:T(8,128)S(1)} %broadcast.274, s32[144]{0:T(256)S(1)} %bitcast.79, f32[144,128,128]{2,1,0:T(8,128)} %copy.29), kind=kCustom, calls=%fused_computation.3.clone.1 | custom fusion | flops 2359296 | bytes 28312128 | tf_op jit(solution)/shard_map/while/body/eval_jaxpr/scatter-add | solution.py:67
  330.9 6.3 gather_fusion.2
  337.3 8.0 %broadcast_multiply_fusion.2 = f32[12,12,128,128]{3,2,1,0:T(8,128)} fusion(f32[12,12]{1,0:T(8,128)S(1)} %fusion.27, bf16[12,12,128,128]{3,2,1,0:T(8,128)(2,1)} %gather_fusion.2, bf16[16,12,128,128]{3,2,1,0:T(8,128)(2,1)} %get-tuple-element.310, s32[]{:T(128)S(6)} %select_n.67), kind=kOutput, calls=%fused_computation.10.clone.1 | convolution fusion | flops 606339072 | bytes 14549572 | tf_op jit(solution)/shard_map/while/body/eval_jaxpr/kcx,klxr->klcr/dot_general | solution.py:62
  345.3 9.6 %copy.29 = f32[144,128,128]{2,1,0:T(8,128)} copy(f32[144,128,128]{1,2,0:T(8,128)} %bitcast.73) | data formatting | bytes 18874368 | tf_op jit(solution)/shard_map/while/body/eval_jaxpr/reshape | solution.py:67
  355.3 19.1 %scatter_fusion = f32[25,128,128]{2,1,0:T(8,128)S(1)} fusion(f32[25,128,128]{2,1,0:T(8,128)S(1)} %broadcast.274, s32[144]{0:T(256)S(1)} %bitcast.79, f32[144,128,128]{2,1,0:T(8,128)} %copy.29), kind=kCustom, calls=%fused_computation.3.clone.1 | custom fusion | flops 2359296 | bytes 28312128 | tf_op jit(solution)/shard_map/while/body/eval_jaxpr/scatter-add | solution.py:67
  392.0 46.8 %all-to-all-done.1 = f32[8,4,8,16,128]{4,3,2,1,0:T(8,128)S(1)} async-done(((f32[8,4,8,16,128]{4,3,2,1,0:T(8,128)}), f32[8,4,8,16,128]{4,3,2,1,0:T(8,128)S(1)}, u32[]{:S(2)}, u32[]{:S(2)}) %all-to-all-start.1) | async-done | bytes 2097184 | tf_op jit(solution)/shard_map/all_to_all | solution.py:45
  443.4 99.3 %all-to-all-done.2 = f32[8,4,17,16,128]{4,3,2,1,0:T(8,128)} async-done(((f32[8,4,17,16,128]{4,3,2,1,0:T(8,128)}), f32[8,4,17,16,128]{4,3,2,1,0:T(8,128)}, u32[]{:S(2)}, u32[]{:S(2)}) %all-to-all-start.2) | async-done | bytes 4456480 | tf_op jit(solution)/shard_map/all_to_all | solution.py:45
  542.7 5.6 pad_maximum_fusion
  548.3 94.4 %while.23 = (s32[]{:T(128)}, bf16[32,25,16,128]{3,2,1,0:T(8,128)(2,1)}, s32[32,25,16,128]{3,2,1,0:T(8,128)}, f32[32,25,16,128]{3,2,1,0:T(8,128)}, s32[]{:T(128)}) while((s32[]{:T(128)}, bf16[32,25,16,128]{3,2,1,0:T(8,128)(2,1)}, s32[32,25,16,128]{3,2,1,0:T(8,128)}, f32[32,25,16,128]{3,2,1,0:T(8,128)}, s32[]{:T(128)}) %tuple.56), condition=%wide.region_5.6_spmd, body=%wide.region_3.5_spmd.sunk | while | flops 512002 | bytes 922433 | solution.py:114
  (194 shorter events, 154.6 us)
Async XLA Ops:
  0.0 13.3 %copy-start.1 = (bf16[32,12,16,128]{3,2,1,0:T(8,128)(2,1)S(1)}, bf16[32,12,16,128]{3,2,1,0:T(8,128)(2,1)}, u32[]{:S(2)}) copy-start(bf16[32,12,16,128]{3,2,1,0:T(8,128)(2,1)} %param.8) | copy-start | bytes 4718596
  1.3 8.0 %collective-permute-start = (bf16[6,12,16,128]{3,2,1,0:T(8,128)(2,1)S(1)}, bf16[6,12,16,128]{3,2,1,0:T(8,128)(2,1)S(1)}, u32[]{:S(2)}, u32[]{:S(2)}) collective-permute-start(bf16[6,12,16,128]{3,2,1,0:T(8,128)(2,1)S(1)} %get-tuple-element.184), channel_id=1, source_target_pairs={{0,1},{1,2},{2,3},{3,4},{4,5},{5,6},{6,7},{7,8},{8,9},{9,10},{10,1... | collective-permute-start | bytes 884744 | tf_op jit(solution)/shard_map/ppermute | solution.py:17
  3.2 14.4 %collective-permute-start.1 = (bf16[6,12,16,128]{3,2,1,0:T(8,128)(2,1)S(1)}, bf16[6,12,16,128]{3,2,1,0:T(8,128)(2,1)S(1)}, u32[]{:S(2)}, u32[]{:S(2)}) collective-permute-start(bf16[6,12,16,128]{3,2,1,0:T(8,128)(2,1)S(1)} %get-tuple-element.183), channel_id=1, source_target_pairs={{1,0},{2,1},{3,2},{4,3},{5,4},{6,5},{7,6},{8,7},{9,8},{10,9},{11,1... | collective-permute-start | bytes 884744 | tf_op jit(solution)/shard_map/ppermute | solution.py:18
  19.7 8.6 %copy-start.2 = (s32[1024,12]{0,1:T(8,128)S(1)}, s32[1024,12]{0,1:T(8,128)}, u32[]{:S(2)}) copy-start(s32[1024,12]{0,1:T(8,128)} %param.9) | copy-start | bytes 147460
  19.7 8.9 %copy-start.3 = (s32[1024]{0:T(1024)S(1)}, s32[1024]{0:T(1024)}, u32[]{:S(2)}) copy-start(s32[1024]{0:T(1024)} %param.10) | copy-start | bytes 12292
  19.7 149.4 %all-to-all-start = ((bf16[8,16,12,16,128]{4,3,2,1,0:T(8,128)(2,1)}), bf16[8,16,12,16,128]{4,3,2,1,0:T(8,128)(2,1)}, u32[]{:S(2)}, u32[]{:S(2)}) async-start(bf16[8,16,12,16,128]{4,3,2,1,0:T(8,128)(2,1)} %fusion.11), calls=%async_computation | async-start | bytes 12582912 | tf_op jit(solution)/shard_map/all_to_all | solution.py:94
  379.3 2.7 copy-start
  383.6 55.2 %all-to-all-start.1 = ((f32[8,4,8,16,128]{4,3,2,1,0:T(8,128)}), f32[8,4,8,16,128]{4,3,2,1,0:T(8,128)S(1)}, u32[]{:S(2)}, u32[]{:S(2)}) async-start(f32[8,4,8,16,128]{4,3,2,1,0:T(8,128)} %split.8), calls=%async_computation.1 | async-start | bytes 4194304 | tf_op jit(solution)/shard_map/all_to_all | solution.py:45
  438.8 103.9 %all-to-all-start.2 = ((f32[8,4,17,16,128]{4,3,2,1,0:T(8,128)}), f32[8,4,17,16,128]{4,3,2,1,0:T(8,128)}, u32[]{:S(2)}, u32[]{:S(2)}) async-start(f32[8,4,17,16,128]{4,3,2,1,0:T(8,128)} %split.9), calls=%async_computation.2 | async-start | bytes 8912896 | tf_op jit(solution)/shard_map/all_to_all | solution.py:45
where the time goes:
time: 647 us; the launch traced here: 643 us
  waiting for transfers between devices  289 us (45%)
  other arithmetic  179 us (28%)
  local copies, waits for them, and re-layouts  112 us (17%)
  matrix products  32.2 us (5%)
  starting transfers between devices  22.4 us (3%)
  loops' own time  8.03 us (1%)
    all_to_all x2, waiting for transfers between devices, exchange_in_pieces(): lax.all_to_all(share, axis, split_axis=0, concat_axis=0, tiled=True)  146 us
    all_to_all x1, waiting for transfers between devices, shards(): lax.all_to_all(windows, 'section', split_axis=0, concat_axis=3, tiled=True)  140 us
    scatter-add x4, other arithmetic, expand(): empty.at[target.reshape(-1)]  76.5 us
    dynamic_update_slice x32, other arithmetic, shards(): return lax.map(one_finish, (back, ranks))  56.6 us
    reshape x4, local copies, waits for them, and re-layouts, expand(): weighted.reshape((slots * slots, columns, rows))  38.3 us
    reduce_sum x32, other arithmetic, finish(): totals = jnp.sum(squared, axis=(0, 2), keepdims=True)  37.5 us
    dot_general x4, matrix products, expand(): jnp.einsum('kcx,klxr->klcr', own, firsts, preferred_element_type=jnp.floa...  32.2 us
    gather x4, local copies, waits for them, and re-layouts, expand(): firsts = banded[where_at]  25.3 us
  transfers between devices with their start and end apart: 5, of which 4 were waited for; matrix products, arithmetic and copies ran while one was open for 2% of the time, Pallas kernels for 0%

commit v1 on v0

--- a/solution.py
+++ b/solution.py
@@ -5,6 +5,30 @@
 
 W = 6
 TOPK = 256
+
+
+def in_blocks(array, dim, size):
+    lengths = array.shape
+    pieces = array.reshape(*lengths[:dim], size, lengths[dim] // size, *lengths[dim + 1 :])
+    return jnp.moveaxis(pieces, dim, 0)
+
+
+def in_order(blocks, dim):
+    lengths = list(blocks.shape[1:])
+    lengths[dim] *= blocks.shape[0]
+    return jnp.moveaxis(blocks, 0, dim).reshape(lengths)
+
+
+def sent_to_each(x, axis, split_dim, concat_dim):
+    devices, index = (lax.axis_size(axis), lax.axis_index(axis))
+    blocks = in_blocks(x, split_dim, devices)
+    filled = blocks
+    for step in range(1, devices):
+        target, source = ((index + step) % devices, (index - step) % devices)
+        sent = lax.dynamic_index_in_dim(blocks, target, 0)
+        other = lax.ppermute(sent, axis, [(i, (i + step) % devices) for i in range(devices)])
+        filled = lax.dynamic_update_slice_in_dim(filled, other, source, axis=0)
+    return in_order(filled, concat_dim)
 
 
 def extended(shard, sides, width):
@@ -91,7 +115,7 @@
     start = first_panel + lax.axis_index("section") * share
     sliced = extended(tiles, (("col", 0),), W)
     windows = jnp.stack([sliced[t * share : t * share + share + 2 * W] for t in range(sections)], 0)
-    whole = lax.all_to_all(windows, "section", split_axis=0, concat_axis=3, tiled=True)[0]
+    whole = sent_to_each(windows, "section", 0, 3)[0]
     win_off = lax.dynamic_slice_in_dim(pad_off, start, share + 2 * W, 0)
     win_cnt = lax.dynamic_slice_in_dim(pad_cnt, start, share + 2 * W, 0)
     loc_off = lax.dynamic_slice_in_dim(offsets, start, share, 0)

time: 647 us -> 654 us (1.011)
  waiting for transfers between devices: 289 us -> 252 us
  starting transfers between devices: 22.4 us -> 52.4 us
  local copies, waits for them, and re-layouts: 112 us -> 124 us
    all_to_all x1 -> x0, waiting for transfers between devices: 140 us -> none  [shards(): lax.all_to_all(windows, 'section', split_axis=0, concat_axis=3, tiled=True)]
    ppermute x0 -> x7, waiting for transfers between devices: none -> 99.5 us  [sent_to_each(): lax.ppermute(sent, axis, [(i, (i + step) % devices) for i in range(device...]
    ppermute x0 -> x7, starting transfers between devices: none -> 34.2 us  [sent_to_each(): lax.ppermute(sent, axis, [(i, (i + step) % devices) for i in range(device...]
    dynamic_update_slice x0 -> x7, local copies, waits for them, and re-layouts: none -> 14 us  [sent_to_each(): filled = lax.dynamic_update_slice_in_dim(filled, other, source, axis=0)]
    all_to_all x1 -> x0, starting transfers between devices: 8.6 us -> none  [shards(): lax.all_to_all(windows, 'section', split_axis=0, concat_axis=3, tiled=True)]
    all_to_all x1 -> x0, local copies, waits for them, and re-layouts: 7.25 us -> none  [shards(): lax.all_to_all(windows, 'section', split_axis=0, concat_axis=3, tiled=True)]
    transpose x0 -> x1, local copies, waits for them, and re-layouts: none -> 7.24 us  [in_order(): return jnp.moveaxis(blocks, 0, dim).reshape(lengths)]
  transfers between devices with their start and end apart: 5 -> 11, of which waited for: 4 -> 9; matrix products, arithmetic and copies ran while one was open for 2% -> 3% of each run, Pallas kernels for 0% -> 0%
where the time goes in v1:
time: 654 us; the launch traced here: 649 us
  waiting for transfers between devices  252 us (39%)
  other arithmetic  180 us (28%)
  local copies, waits for them, and re-layouts  124 us (19%)
  starting transfers between devices  52.4 us (8%)
  matrix products  32.2 us (5%)
  loops' own time  8.16 us (1%)
    all_to_all x2, waiting for transfers between devices, exchange_in_pieces(): lax.all_to_all(share, axis, split_axis=0, concat_axis=0, tiled=True)  150 us
    ppermute x7, waiting for transfers between devices, sent_to_each(): lax.ppermute(sent, axis, [(i, (i + step) % devices) for i in range(device...  99.5 us
    scatter-add x4, other arithmetic, expand(): empty.at[target.reshape(-1)]  76.5 us
    dynamic_update_slice x32, other arithmetic, shards(): return lax.map(one_finish, (back, ranks))  56.6 us
    reshape x4, local copies, waits for them, and re-layouts, expand(): weighted.reshape((slots * slots, columns, rows))  38.3 us
    reduce_sum x32, other arithmetic, finish(): totals = jnp.sum(squared, axis=(0, 2), keepdims=True)  37.5 us
    ppermute x7, starting transfers between devices, sent_to_each(): lax.ppermute(sent, axis, [(i, (i + step) % devices) for i in range(device...  34.2 us
    dot_general x4, matrix products, expand(): jnp.einsum('kcx,klxr->klcr', own, firsts, preferred_element_type=jnp.floa...  32.2 us
  transfers between devices with their start and end apart: 11, of which 9 were waited for; matrix products, arithmetic and copies ran while one was open for 3% of the time, Pallas kernels for 0%

profile of v1, /device:TPU:14, one launch (start us, length us, event | category | flops | bytes accessed | tf_op | source)
XLA Modules:
  0.0 649.3 jit_solution(18236605334195354395)
XLA Ops:
  32.5 7.9 %collective-permute-done.2 = bf16[1,1,16,12,16,128]{5,4,3,2,0,1:T(8,128)(2,1)} collective-permute-done((bf16[1,1,16,12,16,128]{5,4,3,2,0,1:T(8,128)(2,1)}, bf16[1,1,16,12,16,128]{5,4,3,2,0,1:T(8,128)(2,1)}, u32[]{:S(2)}, u32[]{:S(2)}) %collective-permute-start.2) | collective-permute-done | bytes 786464 | tf_op jit(solution)/shard_map/ppermute | solution.py:29
  43.7 17.0 %collective-permute-done.3 = bf16[1,1,16,12,16,128]{5,4,3,2,0,1:T(8,128)(2,1)} collective-permute-done((bf16[1,1,16,12,16,128]{5,4,3,2,0,1:T(8,128)(2,1)}, bf16[1,1,16,12,16,128]{5,4,3,2,0,1:T(8,128)(2,1)}, u32[]{:S(2)}, u32[]{:S(2)}) %collective-permute-start.3) | collective-permute-done | bytes 786464 | tf_op jit(solution)/shard_map/ppermute | solution.py:29
  60.7 16.8 %collective-permute-start.8 = (bf16[1,1,16,12,16,128]{5,4,3,2,0,1:T(8,128)(2,1)S(1)}, bf16[1,1,16,12,16,128]{5,4,3,2,0,1:T(8,128)(2,1)S(1)}, u32[]{:S(2)}, u32[]{:S(2)}) collective-permute-start(bf16[1,1,16,12,16,128]{5,4,3,2,0,1:T(8,128)(2,1)S(1)} %get-tuple-element.183), channel_id=1, source_target_pairs={{0,224},{32,0},{64,32},{96,64},{128,96},{160,128},{192,160},{224,1... | collective-permute-start | bytes 2359304 | tf_op jit(solution)/shard_map/ppermute | solution.py:29
  81.8 42.5 %collective-permute-done.4 = bf16[1,1,16,12,16,128]{5,4,3,2,0,1:T(8,128)(2,1)} collective-permute-done((bf16[1,1,16,12,16,128]{5,4,3,2,0,1:T(8,128)(2,1)}, bf16[1,1,16,12,16,128]{5,4,3,2,0,1:T(8,128)(2,1)}, u32[]{:S(2)}, u32[]{:S(2)}) %collective-permute-start.4) | collective-permute-done | bytes 786464 | tf_op jit(solution)/shard_map/ppermute | solution.py:29
  126.5 16.1 %collective-permute-done.5 = bf16[1,1,16,12,16,128]{5,4,3,2,0,1:T(8,128)(2,1)} collective-permute-done((bf16[1,1,16,12,16,128]{5,4,3,2,0,1:T(8,128)(2,1)S(1)}, bf16[1,1,16,12,16,128]{5,4,3,2,0,1:T(8,128)(2,1)}, u32[]{:S(2)}, u32[]{:S(2)}) %collective-permute-start.5) | collective-permute-done | bytes 786464 | tf_op jit(solution)/shard_map/ppermute | solution.py:29
  154.0 11.1 %collective-permute-done.8 = bf16[1,1,16,12,16,128]{5,4,3,2,0,1:T(8,128)(2,1)S(1)} collective-permute-done((bf16[1,1,16,12,16,128]{5,4,3,2,0,1:T(8,128)(2,1)S(1)}, bf16[1,1,16,12,16,128]{5,4,3,2,0,1:T(8,128)(2,1)S(1)}, u32[]{:S(2)}, u32[]{:S(2)}) %collective-permute-start.8) | collective-permute-done | bytes 786464 | tf_op jit(solution)/shard_map/ppermute | solution.py:29
  166.1 7.2 %copy.20 = bf16[1,16,12,8,16,128]{5,4,3,2,1,0:T(8,128)(2,1)} copy(bf16[1,16,12,8,16,128]{5,4,2,1,3,0:T(8,128)(2,1)} %bitcast.91) | data formatting | bytes 12582912 | tf_op jit(solution)/shard_map/transpose | solution.py:19
  173.3 200.5 %while.22 = (s32[]{:T(128)}, f32[4,25,128,128]{3,2,1,0:T(8,128)}, s32[4,12]{1,0:T(4,128)S(1)}, s32[4]{0:T(128)S(1)}, s32[16,12]{1,0:T(8,128)S(1)}, /*index=5*/bf...) while((s32[]{:T(128)}, f32[4,25,128,128]{3,2,1,0:T(8,128)}, ...), condition=%wide.region_2.3_spmd, body=%wide.region_0.2_spmd.sunk | while | flops 608701376 | bytes 76102056 | solution.py:131
  184.9 8.0 %broadcast_multiply_fusion.2 = f32[12,12,128,128]{3,2,1,0:T(8,128)} fusion(f32[12,12]{1,0:T(8,128)S(1)} %fusion.27, bf16[12,12,128,128]{3,2,1,0:T(8,128)(2,1)} %gather_fusion.2, bf16[16,12,128,128]{3,2,1,0:T(8,128)(2,1)} %get-tuple-element.317, s32[]{:T(128)S(6)} %select_n.197), kind=kOutput, calls=%fused_computation.10.clone.1 | convolution fusion | flops 606339072 | bytes 14549572 | tf_op jit(solution)/shard_map/while/body/eval_jaxpr/kcx,klxr->klcr/dot_general | solution.py:86
  193.0 9.6 %copy.29 = f32[144,128,128]{2,1,0:T(8,128)} copy(f32[144,128,128]{1,2,0:T(8,128)} %bitcast.86) | data formatting | bytes 18874368 | tf_op jit(solution)/shard_map/while/body/eval_jaxpr/reshape | solution.py:91
  203.0 19.1 %scatter_fusion = f32[25,128,128]{2,1,0:T(8,128)S(1)} fusion(f32[25,128,128]{2,1,0:T(8,128)S(1)} %broadcast.288, s32[144]{0:T(256)S(1)} %bitcast.94, f32[144,128,128]{2,1,0:T(8,128)} %copy.29), kind=kCustom, calls=%fused_computation.3.clone.1 | custom fusion | flops 2359296 | bytes 28312128 | tf_op jit(solution)/shard_map/while/body/eval_jaxpr/scatter-add | solution.py:91
  235.0 8.0 %broadcast_multiply_fusion.2 = f32[12,12,128,128]{3,2,1,0:T(8,128)} fusion(f32[12,12]{1,0:T(8,128)S(1)} %fusion.27, bf16[12,12,128,128]{3,2,1,0:T(8,128)(2,1)} %gather_fusion.2, bf16[16,12,128,128]{3,2,1,0:T(8,128)(2,1)} %get-tuple-element.317, s32[]{:T(128)S(6)} %select_n.197), kind=kOutput, calls=%fused_computation.10.clone.1 | convolution fusion | flops 606339072 | bytes 14549572 | tf_op jit(solution)/shard_map/while/body/eval_jaxpr/kcx,klxr->klcr/dot_general | solution.py:86
  243.1 9.6 %copy.29 = f32[144,128,128]{2,1,0:T(8,128)} copy(f32[144,128,128]{1,2,0:T(8,128)} %bitcast.86) | data formatting | bytes 18874368 | tf_op jit(solution)/shard_map/while/body/eval_jaxpr/reshape | solution.py:91
  253.1 19.1 %scatter_fusion = f32[25,128,128]{2,1,0:T(8,128)S(1)} fusion(f32[25,128,128]{2,1,0:T(8,128)S(1)} %broadcast.288, s32[144]{0:T(256)S(1)} %bitcast.94, f32[144,128,128]{2,1,0:T(8,128)} %copy.29), kind=kCustom, calls=%fused_computation.3.clone.1 | custom fusion | flops 2359296 | bytes 28312128 | tf_op jit(solution)/shard_map/while/body/eval_jaxpr/scatter-add | solution.py:91
  285.1 8.0 %broadcast_multiply_fusion.2 = f32[12,12,128,128]{3,2,1,0:T(8,128)} fusion(f32[12,12]{1,0:T(8,128)S(1)} %fusion.27, bf16[12,12,128,128]{3,2,1,0:T(8,128)(2,1)} %gather_fusion.2, bf16[16,12,128,128]{3,2,1,0:T(8,128)(2,1)} %get-tuple-element.317, s32[]{:T(128)S(6)} %select_n.197), kind=kOutput, calls=%fused_computation.10.clone.1 | convolution fusion | flops 606339072 | bytes 14549572 | tf_op jit(solution)/shard_map/while/body/eval_jaxpr/kcx,klxr->klcr/dot_general | solution.py:86
  293.2 9.6 %copy.29 = f32[144,128,128]{2,1,0:T(8,128)} copy(f32[144,128,128]{1,2,0:T(8,128)} %bitcast.86) | data formatting | bytes 18874368 | tf_op jit(solution)/shard_map/while/body/eval_jaxpr/reshape | solution.py:91
  303.2 19.1 %scatter_fusion = f32[25,128,128]{2,1,0:T(8,128)S(1)} fusion(f32[25,128,128]{2,1,0:T(8,128)S(1)} %broadcast.288, s32[144]{0:T(256)S(1)} %bitcast.94, f32[144,128,128]{2,1,0:T(8,128)} %copy.29), kind=kCustom, calls=%fused_computation.3.clone.1 | custom fusion | flops 2359296 | bytes 28312128 | tf_op jit(solution)/shard_map/while/body/eval_jaxpr/scatter-add | solution.py:91
  335.2 8.0 %broadcast_multiply_fusion.2 = f32[12,12,128,128]{3,2,1,0:T(8,128)} fusion(f32[12,12]{1,0:T(8,128)S(1)} %fusion.27, bf16[12,12,128,128]{3,2,1,0:T(8,128)(2,1)} %gather_fusion.2, bf16[16,12,128,128]{3,2,1,0:T(8,128)(2,1)} %get-tuple-element.317, s32[]{:T(128)S(6)} %select_n.197), kind=kOutput, calls=%fused_computation.10.clone.1 | convolution fusion | flops 606339072 | bytes 14549572 | tf_op jit(solution)/shard_map/while/body/eval_jaxpr/kcx,klxr->klcr/dot_general | solution.py:86
  343.3 9.6 %copy.29 = f32[144,128,128]{2,1,0:T(8,128)} copy(f32[144,128,128]{1,2,0:T(8,128)} %bitcast.86) | data formatting | bytes 18874368 | tf_op jit(solution)/shard_map/while/body/eval_jaxpr/reshape | solution.py:91
  353.3 19.1 %scatter_fusion = f32[25,128,128]{2,1,0:T(8,128)S(1)} fusion(f32[25,128,128]{2,1,0:T(8,128)S(1)} %broadcast.288, s32[144]{0:T(256)S(1)} %bitcast.94, f32[144,128,128]{2,1,0:T(8,128)} %copy.29), kind=kCustom, calls=%fused_computation.3.clone.1 | custom fusion | flops 2359296 | bytes 28312128 | tf_op jit(solution)/shard_map/while/body/eval_jaxpr/scatter-add | solution.py:91
  381.6 8.1 %all-to-all-start = ((f32[8,4,8,16,128]{4,3,2,1,0:T(8,128)}), f32[8,4,8,16,128]{4,3,2,1,0:T(8,128)S(1)}, u32[]{:S(2)}, u32[]{:S(2)}) async-start(f32[8,4,8,16,128]{4,3,2,1,0:T(8,128)} %split.8), calls=%async_computation | async-start | bytes 4194304 | tf_op jit(solution)/shard_map/all_to_all | solution.py:69
  394.4 47.9 %all-to-all-done = f32[8,4,8,16,128]{4,3,2,1,0:T(8,128)S(1)} async-done(((f32[8,4,8,16,128]{4,3,2,1,0:T(8,128)}), f32[8,4,8,16,128]{4,3,2,1,0:T(8,128)S(1)}, u32[]{:S(2)}, u32[]{:S(2)}) %all-to-all-start) | async-done | bytes 2097184 | tf_op jit(solution)/shard_map/all_to_all | solution.py:69
  446.9 102.4 %all-to-all-done.1 = f32[8,4,17,16,128]{4,3,2,1,0:T(8,128)} async-done(((f32[8,4,17,16,128]{4,3,2,1,0:T(8,128)}), f32[8,4,17,16,128]{4,3,2,1,0:T(8,128)}, u32[]{:S(2)}, u32[]{:S(2)}) %all-to-all-start.1) | async-done | bytes 4456480 | tf_op jit(solution)/shard_map/all_to_all | solution.py:69
  554.9 94.4 %while.23 = (s32[]{:T(128)}, bf16[32,25,16,128]{3,2,1,0:T(8,128)(2,1)}, s32[32,25,16,128]{3,2,1,0:T(8,128)}, f32[32,25,16,128]{3,2,1,0:T(8,128)}, s32[]{:T(128)}) while((s32[]{:T(128)}, bf16[32,25,16,128]{3,2,1,0:T(8,128)(2,1)}, s32[32,25,16,128]{3,2,1,0:T(8,128)}, f32[32,25,16,128]{3,2,1,0:T(8,128)}, s32[]{:T(128)}) %tuple.62), condition=%wide.region_5.6_spmd, body=%wide.region_3.5_spmd.sunk | while | flops 512002 | bytes 922433 | solution.py:138
  (216 shorter events, 216.8 us)
Async XLA Ops:
  0.0 11.6 %copy-start.2 = (bf16[32,12,16,128]{3,2,1,0:T(8,128)(2,1)S(1)}, bf16[32,12,16,128]{3,2,1,0:T(8,128)(2,1)}, u32[]{:S(2)}) copy-start(bf16[32,12,16,128]{3,2,1,0:T(8,128)(2,1)} %param.8) | copy-start | bytes 4718596
  1.3 8.0 %collective-permute-start = (bf16[6,12,16,128]{3,2,1,0:T(8,128)(2,1)S(1)}, bf16[6,12,16,128]{3,2,1,0:T(8,128)(2,1)S(1)}, u32[]{:S(2)}, u32[]{:S(2)}) collective-permute-start(bf16[6,12,16,128]{3,2,1,0:T(8,128)(2,1)S(1)} %get-tuple-element.191), channel_id=1, source_target_pairs={{0,1},{1,2},{2,3},{3,4},{4,5},{5,6},{6,7},{7,8},{8,9},{9,10},{10,1... | collective-permute-start | bytes 884744 | tf_op jit(solution)/shard_map/ppermute | solution.py:41
  3.2 9.2 %collective-permute-start.1 = (bf16[6,12,16,128]{3,2,1,0:T(8,128)(2,1)S(1)}, bf16[6,12,16,128]{3,2,1,0:T(8,128)(2,1)S(1)}, u32[]{:S(2)}, u32[]{:S(2)}) collective-permute-start(bf16[6,12,16,128]{3,2,1,0:T(8,128)(2,1)S(1)} %get-tuple-element.190), channel_id=1, source_target_pairs={{1,0},{2,1},{3,2},{4,3},{5,4},{6,5},{7,6},{8,7},{9,8},{10,9},{11,1... | collective-permute-start | bytes 884744 | tf_op jit(solution)/shard_map/ppermute | solution.py:42
  12.6 19.7 %copy-start.3 = (s32[1024,12]{0,1:T(8,128)S(1)}, s32[1024,12]{0,1:T(8,128)}, u32[]{:S(2)}) copy-start(s32[1024,12]{0,1:T(8,128)} %param.9) | copy-start | bytes 147460
  12.7 30.6 %copy-start.4 = (s32[1024]{0:T(1024)S(1)}, s32[1024]{0:T(1024)}, u32[]{:S(2)}) copy-start(s32[1024]{0:T(1024)} %param.10) | copy-start | bytes 12292
  12.9 2.7 copy-start.1
  17.6 22.7 %collective-permute-start.2 = (bf16[1,1,16,12,16,128]{5,4,3,2,0,1:T(8,128)(2,1)}, bf16[1,1,16,12,16,128]{5,4,3,2,0,1:T(8,128)(2,1)}, u32[]{:S(2)}, u32[]{:S(2)}) collective-permute-start(bf16[1,1,16,12,16,128]{5,4,3,2,0,1:T(8,128)(2,1)} %get-tuple-element.189), channel_id=1, source_target_pairs={{0,32},{32,64},{64,96},{96,128},{128,160},{160,192},{192,224},{224... | collective-permute-start | bytes 2359304 | tf_op jit(solution)/shard_map/ppermute | solution.py:29
  19.6 41.1 %collective-permute-start.3 = (bf16[1,1,16,12,16,128]{5,4,3,2,0,1:T(8,128)(2,1)}, bf16[1,1,16,12,16,128]{5,4,3,2,0,1:T(8,128)(2,1)}, u32[]{:S(2)}, u32[]{:S(2)}) collective-permute-start(bf16[1,1,16,12,16,128]{5,4,3,2,0,1:T(8,128)(2,1)} %get-tuple-element.188), channel_id=1, source_target_pairs={{0,64},{32,96},{64,128},{96,160},{128,192},{160,224},{192,0},{224,... | collective-permute-start | bytes 2359304 | tf_op jit(solution)/shard_map/ppermute | solution.py:29
  22.8 101.5 %collective-permute-start.4 = (bf16[1,1,16,12,16,128]{5,4,3,2,0,1:T(8,128)(2,1)}, bf16[1,1,16,12,16,128]{5,4,3,2,0,1:T(8,128)(2,1)}, u32[]{:S(2)}, u32[]{:S(2)}) collective-permute-start(bf16[1,1,16,12,16,128]{5,4,3,2,0,1:T(8,128)(2,1)} %get-tuple-element.187), channel_id=1, source_target_pairs={{0,96},{32,128},{64,160},{96,192},{128,224},{160,0},{192,32},{224,... | collective-permute-start | bytes 2359304 | tf_op jit(solution)/shard_map/ppermute | solution.py:29
  26.9 115.7 %collective-permute-start.5 = (bf16[1,1,16,12,16,128]{5,4,3,2,0,1:T(8,128)(2,1)S(1)}, bf16[1,1,16,12,16,128]{5,4,3,2,0,1:T(8,128)(2,1)}, u32[]{:S(2)}, u32[]{:S(2)}) collective-permute-start(bf16[1,1,16,12,16,128]{5,4,3,2,0,1:T(8,128)(2,1)S(1)} %get-tuple-element.186), channel_id=1, source_target_pairs={{0,128},{32,160},{64,192},{96,224},{128,0},{160,32},{192,64},{224,... | collective-permute-start | bytes 2359304 | tf_op jit(solution)/shard_map/ppermute | solution.py:29
  27.4 117.4 %collective-permute-start.6 = (bf16[1,1,16,12,16,128]{5,4,3,2,0,1:T(8,128)(2,1)S(1)}, bf16[1,1,16,12,16,128]{5,4,3,2,0,1:T(8,128)(2,1)}, u32[]{:S(2)}, u32[]{:S(2)}) collective-permute-start(bf16[1,1,16,12,16,128]{5,4,3,2,0,1:T(8,128)(2,1)S(1)} %get-tuple-element.185), channel_id=1, source_target_pairs={{0,160},{32,192},{64,224},{96,0},{128,32},{160,64},{192,96},{224,1... | collective-permute-start | bytes 2359304 | tf_op jit(solution)/shard_map/ppermute | solution.py:29
  40.4 111.4 %collective-permute-start.7 = (bf16[1,1,16,12,16,128]{5,4,3,2,0,1:T(8,128)(2,1)S(1)}, bf16[1,1,16,12,16,128]{5,4,3,2,0,1:T(8,128)(2,1)}, u32[]{:S(2)}, u32[]{:S(2)}) collective-permute-start(bf16[1,1,16,12,16,128]{5,4,3,2,0,1:T(8,128)(2,1)S(1)} %get-tuple-element.184), channel_id=1, source_target_pairs={{0,192},{32,224},{64,0},{96,32},{128,64},{160,96},{192,128},{224,1... | collective-permute-start | bytes 2359304 | tf_op jit(solution)/shard_map/ppermute | solution.py:29
  60.7 104.4 %collective-permute-start.8 = (bf16[1,1,16,12,16,128]{5,4,3,2,0,1:T(8,128)(2,1)S(1)}, bf16[1,1,16,12,16,128]{5,4,3,2,0,1:T(8,128)(2,1)S(1)}, u32[]{:S(2)}, u32[]{:S(2)}) collective-permute-start(bf16[1,1,16,12,16,128]{5,4,3,2,0,1:T(8,128)(2,1)S(1)} %get-tuple-element.183), channel_id=1, source_target_pairs={{0,224},{32,0},{64,32},{96,64},{128,96},{160,128},{192,160},{224,1... | collective-permute-start | bytes 2359304 | tf_op jit(solution)/shard_map/ppermute | solution.py:29
  377.3 2.7 copy-start
  381.6 60.7 %all-to-all-start = ((f32[8,4,8,16,128]{4,3,2,1,0:T(8,128)}), f32[8,4,8,16,128]{4,3,2,1,0:T(8,128)S(1)}, u32[]{:S(2)}, u32[]{:S(2)}) async-start(f32[8,4,8,16,128]{4,3,2,1,0:T(8,128)} %split.8), calls=%async_computation | async-start | bytes 4194304 | tf_op jit(solution)/shard_map/all_to_all | solution.py:69
  442.3 107.0 %all-to-all-start.1 = ((f32[8,4,17,16,128]{4,3,2,1,0:T(8,128)}), f32[8,4,17,16,128]{4,3,2,1,0:T(8,128)}, u32[]{:S(2)}, u32[]{:S(2)}) async-start(f32[8,4,17,16,128]{4,3,2,1,0:T(8,128)} %split.9), calls=%async_computation.1 | async-start | bytes 8912896 | tf_op jit(solution)/shard_map/all_to_all | solution.py:69
